TPU v7x, 32 devices: a whole 2x2x4 slice. The times are simulated.
32 devices in a mesh: dp: 8 (over y, x, core), vocab: 4 (over z).
Axes of the slice: x: 2, y: 2, z: 4, core: 2. Of those that a mesh axis runs over, the one named last changes fastest.
Arguments:
- resid: bfloat16 [2, 1024, 4096], P(None, 'dp'), may hold values from -6 to 6
- norm_gain: float32 [4096], replicated, may hold values from 0.5 to 1.5
- in_x: bfloat16 [4096, 4096], P('dp', 'vocab'), may hold values from -0.09375 to 0.09375
- in_z: bfloat16 [4096, 4096], P('dp', 'vocab'), may hold values from -0.09375 to 0.09375
- conv_w: float32 [4, 4096], P(None, 'vocab'), may hold values from -3 to 3
- conv_b: float32 [4096], P('vocab'), may hold values from -3 to 3
- xdt_w: bfloat16 [4096, 256], P('vocab'), may hold values from -0.09375 to 0.09375
- xbc_w: bfloat16 [4096, 32], P('vocab'), may hold values from -0.09375 to 0.09375
- dt_gain: float32 [256], replicated, may hold values from 0.5 to 1.5
- dt_proj: bfloat16 [256, 4096], P(None, 'vocab'), may hold values from -0.375 to 0.375
- dt_bias: float32 [4096], P('vocab'), may hold values from -4 to 1
- a_rate: float32 [4096, 16], P('vocab'), may hold values from 0.0001 to 1
- out_w: bfloat16 [4096, 4096], P('vocab'), may hold values from -0.09375 to 0.09375
- final_gain: float32 [4096], replicated, may hold values from 0.5 to 1.5
- head_w: bfloat16 [8192, 4096], P('vocab', 'dp'), as said below
- targets: int32 [2, 1024], P(None, 'dp'), may hold values from 0 to 8191
- lengths: int32 [2], replicated, may hold values from 256 to 1024
Outputs:
- hidden_out: bfloat16 [2, 1024, 4096], P(None, 'dp', 'vocab')
- token_logp: float32 [2, 1024], P(None, 'dp')
- mean_logp: float32 [], replicated
Inputs may be any that keep to these rules, and one draw needn't show every extreme that they name: `head_w`: entries lie within 720 / sqrt(4096) of zero.
All inputs are finite; a program needn't handle non-finite values.
Results may differ from a plain program's by a relative error of at most 0.019.
Values may be sent and summed in bfloat16 or wider, within the bound.
A program may use at most 128 MiB of HBM per device.

v0:
```python
import math
import jax
import jax.numpy as jnp
from jax import lax
from jax.sharding import PartitionSpec as P


def shifted(array, axis, by):
    peers = lax.axis_size(axis)
    pairs = [(i, i + by) for i in range(peers) if 0 <= i + by < peers]
    return lax.ppermute(array, axis, pairs)


def prefix(part, axis, combine, identity):
    place = lax.axis_index(axis)
    gathered = jax.tree.map(lambda a: lax.all_gather(a, axis), part)
    state = jax.tree.map(lambda a, e: jnp.zeros_like(a) + jnp.asarray(e, a.dtype), part, identity)

    def one(step, state):
        return combine(
            state, jax.tree.map(lambda a: lax.dynamic_index_in_dim(a, step, 0, False), gathered)
        )

    return lax.fori_loop(0, place, one, state)


def rms_norm(values, gain, epsilon):
    return values * lax.rsqrt(jnp.mean(values * values, axis=-1, keepdims=True) + epsilon) * gain


def head_logits(final, head_w):
    return lax.dot_general(
        final,
        lax.all_gather(head_w, "dp", axis=1, tiled=True),
        (((1,), (1,)), ((), ())),
        preferred_element_type=jnp.float32,
    )


def body(
    resid,
    norm_gain,
    in_x,
    in_z,
    conv_w,
    conv_b,
    xdt_w,
    xbc_w,
    dt_gain,
    dt_proj,
    dt_bias,
    a_rate,
    out_w,
    final_gain,
    head_w,
    targets,
    lengths,
):
    batch_count, local_len, width = resid.shape
    channels = in_x.shape[1]
    nstate = a_rate.shape[1]
    kernel_len = conv_w.shape[0]
    row_count = batch_count * local_len
    stream = resid.astype(jnp.float32)
    normed = rms_norm(stream, norm_gain, 1e-05).astype(jnp.bfloat16).reshape(row_count, width)
    x_acc = jnp.dot(
        normed, lax.all_gather(in_x, "dp", axis=0, tiled=True), preferred_element_type=jnp.float32
    )
    z_acc = jnp.dot(
        normed, lax.all_gather(in_z, "dp", axis=0, tiled=True), preferred_element_type=jnp.float32
    )
    x_inner = x_acc.astype(jnp.bfloat16).reshape(batch_count, local_len, channels)
    z_gate = z_acc.astype(jnp.bfloat16).reshape(batch_count, local_len, channels)
    before = shifted(x_inner[:, local_len - (kernel_len - 1) :, :], "dp", 1)
    padded = jnp.concatenate([before, x_inner], axis=1).astype(jnp.float32)
    conv_sum = jnp.zeros((batch_count, local_len, channels), jnp.float32) + conv_b
    for tap_index in range(kernel_len):
        conv_sum = conv_sum + conv_w[tap_index] * padded[:, tap_index : tap_index + local_len, :]
    conv_act = jax.nn.silu(conv_sum)
    conv_low = conv_act.astype(jnp.bfloat16).reshape(row_count, channels)
    dt_raw, bc_raw = (
        lax.psum(
            jnp.dot(conv_low, xdt_w, preferred_element_type=jnp.float32).astype(jnp.bfloat16),
            "vocab",
        ).astype(jnp.float32),
        lax.psum(
            jnp.dot(conv_low, xbc_w, preferred_element_type=jnp.float32).astype(jnp.bfloat16),
            "vocab",
        ).astype(jnp.float32),
    )
    dt_normed = rms_norm(dt_raw, dt_gain, 1e-06).astype(jnp.bfloat16)
    step_size = jax.nn.softplus(
        jnp.dot(dt_normed, dt_proj, preferred_element_type=jnp.float32) + dt_bias
    ).reshape(batch_count, local_len, channels)
    in_map = bc_raw[:, :nstate].reshape(batch_count, local_len, nstate)
    out_map = bc_raw[:, nstate:].reshape(batch_count, local_len, nstate)
    block_len = math.gcd(local_len, 16)
    block_count = local_len // block_len

    def by_block(values):
        return values.transpose(1, 0, 2).reshape(
            (block_count, block_len) + (values.shape[0], values.shape[2])
        )

    def run_block(carry_state, inputs):
        step_blk, conv_blk, in_blk, out_blk = inputs
        results = []
        for position in range(block_len):
            carry_state = (
                jnp.exp(-step_blk[position][..., None] * a_rate) * carry_state
                + (step_blk[position] * conv_blk[position])[..., None]
                * in_blk[position][:, None, :]
            )
            results.append(jnp.sum(carry_state * out_blk[position][:, None, :], axis=-1))
        return (carry_state, jnp.stack(results))

    start_state = jnp.zeros((batch_count, channels, nstate), jnp.float32)
    last_state, local_out = lax.scan(
        run_block,
        start_state,
        (by_block(step_size), by_block(conv_act), by_block(in_map), by_block(out_map)),
    )
    local_out = local_out.reshape(local_len, batch_count, channels).transpose(1, 0, 2)
    step_total = jnp.sum(step_size, axis=1)
    last_decay = jnp.exp(-step_total[..., None] * a_rate)

    def chain(earlier, later):
        return (earlier[0] * later[0], later[0] * earlier[1] + later[1])

    _, state_in = prefix(
        (last_decay, last_state),
        "dp",
        chain,
        (jnp.ones_like(last_decay), jnp.zeros_like(last_state)),
    )
    step_cumul = jnp.cumsum(step_size, axis=1)
    carried = jnp.sum(
        out_map[:, :, None, :] * jnp.exp(-step_cumul[..., None] * a_rate) * state_in[:, None, :, :],
        axis=-1,
    )
    mixed = local_out + carried
    gated = (
        (mixed * jax.nn.silu(z_gate.astype(jnp.float32)))
        .astype(jnp.bfloat16)
        .reshape(row_count, channels)
    )
    partial_value = jnp.dot(gated, out_w, preferred_element_type=jnp.float32)
    vocab_count = lax.axis_size("vocab")
    vocab_index = lax.axis_index("vocab")
    share_width = width // vocab_count
    flat_stream = stream.reshape(row_count, width)
    mixer_out = lax.psum(partial_value.astype(jnp.bfloat16), "vocab").astype(jnp.float32)
    hidden = (flat_stream + mixer_out).astype(jnp.bfloat16)
    final = rms_norm(hidden.astype(jnp.float32), final_gain, 1e-05).astype(jnp.bfloat16)
    hidden_share = lax.dynamic_slice_in_dim(hidden, vocab_index * share_width, share_width, 1)
    logits = head_logits(final, head_w)
    vocab_rows = head_w.shape[0]
    local_ids = targets.reshape(row_count) - vocab_index * vocab_rows
    entry_ids = lax.broadcasted_iota(jnp.int32, (row_count, vocab_rows), 1)
    picked = jnp.sum(jnp.where(entry_ids == local_ids[:, None], logits, 0.0), axis=-1)
    local_top = jnp.max(logits, axis=-1)
    global_top = lax.pmax(local_top, "vocab")
    exp_local = jnp.sum(jnp.exp(logits - global_top[:, None]), axis=-1)
    exp_total, picked_all = lax.psum((exp_local, picked), "vocab")
    log_total = global_top + jnp.log(exp_total)
    token_logp = (picked_all - log_total).reshape(batch_count, local_len)
    positions = lax.axis_index("dp") * local_len + jnp.arange(local_len, dtype=jnp.int32)
    valid_mask = positions[None, :] < lengths[:, None]
    masked_sum = jnp.sum(jnp.where(valid_mask, token_logp, 0.0))
    grand_sum = lax.psum(masked_sum, "dp")
    mean_logp = grand_sum / jnp.sum(lengths.astype(jnp.float32))
    return (hidden_share.reshape(batch_count, local_len, share_width), token_logp, mean_logp)


def solution(mesh):
    in_specs = (
        P(None, "dp", None),
        P(),
        P("dp", "vocab"),
        P("dp", "vocab"),
        P(None, "vocab"),
        P("vocab"),
        P("vocab", None),
        P("vocab", None),
        P(),
        P(None, "vocab"),
        P("vocab"),
        P("vocab", None),
        P("vocab", None),
        P(),
        P("vocab", "dp"),
        P(None, "dp"),
        P(),
    )
    out_specs = (P(None, "dp", "vocab"), P(None, "dp"), P())
    return jax.shard_map(body, mesh=mesh, in_specs=in_specs, out_specs=out_specs, check_vma=False)
```

profile of v0, /device:TPU:0, one launch (start us, length us, event | category | flops | bytes accessed | tf_op | source)
XLA Modules:
  0.0 477.5 jit_solution(16889401138438752080)
XLA Ops:
  8.0 2.1 multiply_reduce_fusion.17
  10.1 2.7 multiply_convert_fusion
  12.8 54.1 %all-gather.7.cloned.1.call-done = bf16[4096,1024]{1,0:T(8,128)(2,1)} async-done(((bf16[512,1024]{1,0:T(8,128)(2,1)}), bf16[4096,1024]{1,0:T(8,128)(2,1)}) %all-gather.7.cloned.1.call-update) | async-done | bytes 8388624 | tf_op jit(solution)/shard_map/all_gather | solution.py:67
  66.9 6.4 %convolution_convert_fusion.2 = bf16[256,1024]{1,0:T(8,128)(2,1)S(1)} fusion(bf16[256,4096]{1,0:T(8,128)(2,1)} %bitcast.279, bf16[4096,1024]{1,0:T(8,128)(2,1)} %all-gather.7.cloned.1.call-done), kind=kOutput, calls=%fused_computation.218 | convolution fusion | flops 2147745792 | bytes 11010048 | tf_op jit(solution)/shard_map/dot_general | solution.py:66
  73.3 2.3 collective-permute-start
  75.6 0.8 collective-permute-done
  76.6 1.7 fusion.75
  78.3 1.0 convolution_convert_fusion.3
  80.3 18.7 %psum.43 = bf16[256,32]{0,1:T(8,128)(2,1)S(1)} all-reduce(bf16[256,32]{0,1:T(8,128)(2,1)S(1)} %convolution_convert_fusion.4), channel_id=1, replica_groups=mesh['dp'=8,'vocab'=4] {'vocab'}, use_global_device_ids=true, to_apply=%region_3.4 | all-reduce | flops 8192 | bytes 32768 | tf_op jit(solution)/shard_map/psum | solution.py:86
  99.4 17.4 %all-reduce.4.cloned.1.call-done = bf16[256,256]{1,0:T(8,128)(2,1)} async-done(((bf16[256,256]{1,0:T(8,128)(2,1)}), bf16[256,256]{1,0:T(8,128)(2,1)}) %all-reduce.4.cloned.1.call-update) | async-done | bytes 131088 | tf_op jit(solution)/shard_map/psum | solution.py:82
  116.7 1.0 fusion.66
  117.8 1.8 bitcast_reduce_fusion
  119.6 1.0 copy-done.5
  120.5 1.9 copy.36
  122.4 48.8 %while.26 = (s32[]{:T(128)}, f32[2,1024,16]{1,2,0:T(8,128)S(1)}, f32[8,16,2,1024]{3,1,0,2:T(8,128)}, f32[8,16,2,1024]{3,2,1,0:T(2,128)}, f32[1024,16]{0,1:T(8,12...) while((s32[]{:T(128)}, f32[2,1024,16]{1,2,0:T(8,128)S(1)}, ...), condition=%wide.region_21.22_spmd.clone, body=%wide.region_4.21_spmd.clone.sunk | while | flops 4816914 | bytes 3422816 | solution.py:118
  122.4 1.6 constant_dynamic-slice_fusion.66
  124.0 0.9 negate_bitcast_fusion.18
  125.0 1.0 negate_bitcast_fusion.19
  128.5 1.6 constant_dynamic-slice_fusion.66
  130.2 0.9 negate_bitcast_fusion.18
  131.1 1.0 negate_bitcast_fusion.19
  133.9 0.7 copy_dynamic-update-slice_fusion.2
  134.6 1.6 constant_dynamic-slice_fusion.66
  136.2 0.9 negate_bitcast_fusion.18
  137.1 1.0 negate_bitcast_fusion.19
  140.0 0.7 copy_dynamic-update-slice_fusion.2
  140.7 1.6 constant_dynamic-slice_fusion.66
  142.3 0.9 negate_bitcast_fusion.18
  143.2 1.0 negate_bitcast_fusion.19
  146.0 0.7 copy_dynamic-update-slice_fusion.2
  146.7 1.6 constant_dynamic-slice_fusion.66
  148.3 0.9 negate_bitcast_fusion.18
  149.2 1.0 negate_bitcast_fusion.19
  152.1 0.7 copy_dynamic-update-slice_fusion.2
  152.8 1.6 constant_dynamic-slice_fusion.66
  154.4 0.9 negate_bitcast_fusion.18
  155.3 1.0 negate_bitcast_fusion.19
  158.2 0.7 copy_dynamic-update-slice_fusion.2
  158.8 1.9 constant_dynamic-slice_fusion.66
  160.7 0.9 negate_bitcast_fusion.18
  161.6 1.0 negate_bitcast_fusion.19
  164.5 0.7 copy_dynamic-update-slice_fusion.2
  165.2 1.6 constant_dynamic-slice_fusion.66
  166.8 0.9 negate_bitcast_fusion.18
  167.7 1.0 negate_bitcast_fusion.19
  170.5 0.7 copy_dynamic-update-slice_fusion.2
  172.7 6.3 %convolution_convert_fusion.1 = bf16[256,1024]{1,0:T(8,128)(2,1)S(1)} fusion(bf16[256,4096]{1,0:T(8,128)(2,1)} %bitcast.280, bf16[4096,1024]{1,0:T(8,128)(2,1)} %all-gather.11.cloned.1.call-done), kind=kOutput, calls=%fused_computation.217 | convolution fusion | flops 2147745792 | bytes 11010048 | tf_op jit(solution)/shard_map/dot_general | solution.py:69
  179.2 2.7 reduce_window_sum.11
  181.9 2.3 neg.205
  184.3 13.5 %all-gather.15.cloned.1.call-done = f32[16,1024,16]{1,2,0:T(8,128)} async-done(((f32[2,1024,16]{1,2,0:T(8,128)}), f32[16,1024,16]{1,2,0:T(8,128)}) %all-gather.15.cloned.1.call-update) | async-done | bytes 1048592 | tf_op jit(solution)/shard_map/all_gather | solution.py:16
  197.8 25.7 %all-gather.9.cloned.1.call-done = f32[8,2,1024,16]{2,3,1,0:T(8,128)} async-done(((f32[1,2,1024,16]{2,3,1,0:T(8,128)}), f32[8,2,1024,16]{2,3,1,0:T(8,128)}) %all-gather.9.cloned.1.call-update) | async-done | bytes 1048592 | tf_op jit(solution)/shard_map/all_gather | solution.py:16
  223.7 6.2 %multiply_reduce_fusion.16 = f32[2,128,1024]{2,1,0:T(8,128)S(1)} fusion(f32[2,1024,16]{1,2,0:T(8,128)S(1)} %get-tuple-element.92, f32[1024,16]{0,1:T(8,128)S(1)} %get-tuple-element.677, f32[2,128,1024]{2,1,0:T(8,128)} %neg.205, f32[2,128,16]{2,1,0:T(8,128)S(1)} %copy.41), kind=kLoop, calls=%fused_computation.196 | loop fusion | flops 16515072 | bytes 2310144 | tf_op jit(solution)/shard_map/reduce_sum | solution.py:137
  230.3 7.0 %convolution_convert_fusion = bf16[256,4096]{1,0:T(8,128)(2,1)} fusion(bf16[256,1024]{1,0:T(8,128)(2,1)S(1)} %bitcast.285, bf16[1024,4096]{1,0:T(8,128)(2,1)} %param.33), kind=kOutput, calls=%fused_computation.199 | convolution fusion | flops 2148532224 | bytes 11010048 | tf_op jit(solution)/shard_map/dot_general | solution.py:147
  237.4 0.7 all-gather.13.cloned.1.call-update
  238.8 92.2 %all-reduce.6.cloned.1.call-done = bf16[256,4096]{1,0:T(8,128)(2,1)} async-done(((bf16[256,4096]{1,0:T(8,128)(2,1)}), bf16[256,4096]{1,0:T(8,128)(2,1)}) %all-reduce.6.cloned.1.call-update) | async-done | bytes 2097168 | tf_op jit(solution)/shard_map/psum | solution.py:152
  331.0 2.5 fusion.49
  333.5 1.3 copy-done.6
  334.9 0.8 constant_dynamic-slice_fusion.64
  335.7 89.2 %all-gather.13.cloned.1.call-done = bf16[2048,4096]{1,0:T(8,128)(2,1)} async-done(((bf16[2048,512]{1,0:T(8,128)(2,1)}), bf16[2048,4096]{1,0:T(8,128)(2,1)}) %all-gather.13.cloned.1.call-update) | async-done | bytes 16777232 | tf_op jit(solution)/shard_map/all_gather | solution.py:34
  424.9 9.0 %fusion.78 = (f32[256]{0:T(256)S(1)}, f32[256,2048]{1,0:T(8,128)S(1)}) fusion(bf16[2048,4096]{1,0:T(8,128)(2,1)} %all-gather.13.cloned.1.call-done, bf16[256,4096]{1,0:T(8,128)(2,1)} %copy-done.6, f32[4096]{0:T(1024)S(1)} %copy-done.14, f32[256]{0:T(256)S(1)} %add_rsqrt_fusion), kind=kOutput, calls=%fused_computation.260 | convolution fusion | flops 4299685888 | bytes 20989952 | tf_op jit(solution)/shard_map/dot_general | solution.py:32
  433.9 11.7 %pmax.7 = f32[256]{0:T(256)S(1)} all-reduce(f32[256]{0:T(256)S(1)} %get-tuple-element.288), channel_id=1, replica_groups=mesh['dp'=8,'vocab'=4] {'vocab'}, use_global_device_ids=true, to_apply=%region_32.33 | all-reduce | flops 256 | bytes 2048 | tf_op jit(solution)/shard_map/pmax | solution.py:162
  446.2 8.4 %all-reduce = (f32[256]{0:T(256)S(1)}, f32[256]{0:T(256)S(1)}) all-reduce(f32[256]{0:T(256)S(1)} %get-tuple-element.144, f32[256]{0:T(256)S(1)} %get-tuple-element.143), channel_id=1, replica_groups=mesh['dp'=8,'vocab'=4] {'vocab'}, use_global_device_ids=true, to_apply=%region_30.31 | all-reduce | flops 512 | bytes 4096 | tf_op jit(solution)/shard_map/psum | solution.py:164
  454.7 1.2 fusion.72
  455.8 12.4 %psum.47 = f32[]{:T(128)} all-reduce(f32[]{:T(128)} %get-tuple-element.284), channel_id=1, replica_groups=mesh['dp'=8,'vocab'=4] {'dp'}, use_global_device_ids=true, to_apply=%region_36.37 | all-reduce | flops 1 | bytes 8 | tf_op jit(solution)/shard_map/psum | solution.py:170
  (247 shorter events, 20.8 us)
Async XLA Ops:
  7.2 110.6 %copy-start = (bf16[256,1024]{1,0:T(8,128)(2,1)S(1)}, bf16[256,1024]{1,0:T(8,128)(2,1)}, u32[]{:S(2)}) copy-start(bf16[256,1024]{1,0:T(8,128)(2,1)} %param.30) | copy-start | bytes 1572868
  7.2 2.9 copy-start.3
  7.2 59.7 %all-gather.7.cloned.1.call-start = ((), (), s32[]{:S(2)}) async-start(), calls=%async_computation | async-start | bytes 9437184 | tf_op jit(solution)/shard_map/all_gather | solution.py:67
  7.9 108.8 %all-reduce.4.cloned.1.call-start = ((), (), s32[]{:S(2)}) async-start(), calls=%async_computation.1 | async-start | bytes 262144 | tf_op jit(solution)/shard_map/psum | solution.py:82
  66.9 8.7 %copy-start.10 = (f32[4,1024]{1,0:T(4,128)S(1)}, f32[4,1024]{1,0:T(4,128)}, u32[]{:S(2)}) copy-start(f32[4,1024]{1,0:T(4,128)} %param.25) | copy-start | bytes 49156
  66.9 9.7 %copy-start.11 = (f32[1024]{0:T(1024)S(1)}, f32[1024]{0:T(1024)}, u32[]{:S(2)}) copy-start(f32[1024]{0:T(1024)} %param.26) | copy-start | bytes 12292
  73.3 5.0 %copy-start.8 = (bf16[1024,256]{1,0:T(8,128)(2,1)S(1)}, bf16[1024,256]{1,0:T(8,128)(2,1)}, u32[]{:S(2)}) copy-start(bf16[1024,256]{1,0:T(8,128)(2,1)} %param.27) | copy-start | bytes 1572868
  73.3 3.1 collective-permute-start
  76.6 3.5 copy-start.9
  76.6 41.2 %copy-start.15 = (f32[1024]{0:T(1024)S(1)}, f32[1024]{0:T(1024)}, u32[]{:S(2)}) copy-start(f32[1024]{0:T(1024)} %param.31) | copy-start | bytes 12292
  76.6 41.2 %copy-start.16 = (f32[256]{0:T(256)S(1)}, f32[256]{0:T(256)}, u32[]{:S(2)}) copy-start(f32[256]{0:T(256)} %param.29) | copy-start | bytes 3076
  79.3 43.2 %copy-start.2 = (f32[1024,16]{0,1:T(8,128)S(1)}, f32[1024,16]{0,1:T(8,128)}, u32[]{:S(2)}) copy-start(f32[1024,16]{0,1:T(8,128)} %param.32) | copy-start | bytes 196612
  79.3 93.4 %all-gather.11.cloned.1.call-start = ((), (), s32[]{:S(2)}) async-start(), calls=%async_computation.3 | async-start | bytes 9437184 | tf_op jit(solution)/shard_map/all_gather | solution.py:70
  80.0 117.7 %all-gather.15.cloned.1.call-start = ((), (), s32[]{:S(2)}) async-start(), calls=%async_computation.6 | async-start | bytes 1179648 | tf_op jit(solution)/shard_map/all_gather | solution.py:16
  119.6 1.0 copy-start.5
  171.2 0.6 copy-start.4
  171.9 51.6 %all-gather.9.cloned.1.call-start = ((), (), s32[]{:S(2)}) async-start(), calls=%async_computation.2 | async-start | bytes 1179648 | tf_op jit(solution)/shard_map/all_gather | solution.py:16
  172.6 158.3 %all-reduce.6.cloned.1.call-start = ((), (), s32[]{:S(2)}) async-start(), calls=%async_computation.4 | async-start | bytes 4194304 | tf_op jit(solution)/shard_map/psum | solution.py:152
  223.7 6.3 %copy-start.7 = (f32[8,16,2,1024]{3,1,0,2:T(8,128)S(1)}, f32[8,16,2,1024]{3,1,0,2:T(8,128)}, u32[]{:S(2)}) copy-start(f32[8,16,2,1024]{3,1,0,2:T(8,128)} %get-tuple-element.90) | copy-start | bytes 3145732
  237.3 0.8 copy-start.13
  237.3 1.5 copy-start.12
  237.4 187.6 %all-gather.13.cloned.1.call-start = ((), (), s32[]{:S(2)}) async-start(), calls=%async_computation.5 | async-start | bytes 18874368 | tf_op jit(solution)/shard_map/all_gather | solution.py:34
  238.1 186.8 %copy-start.14 = (f32[4096]{0:T(1024)S(1)}, f32[4096]{0:T(1024)}, u32[]{:S(2)}) copy-start(f32[4096]{0:T(1024)} %param.34) | copy-start | bytes 49156
  333.5 1.4 copy-start.6
  424.9 44.6 %copy-start.1 = (bf16[256,1024]{1,0:T(8,128)(2,1)S(1)}, bf16[256,1024]{1,0:T(8,128)(2,1)}, u32[]{:S(2)}) copy-start(bf16[256,1024]{1,0:T(8,128)(2,1)} %param.30) | copy-start | bytes 1572868
Sparse Core Ops, SparseCore 0:
  9.9 56.9 all-gather.6
  79.4 37.2 all-reduce.3
  118.6 53.9 all-gather.10
  174.4 23.3 all-gather.14
  200.1 23.3 all-gather.8
  237.5 93.4 all-reduce.5
  332.8 92.0 all-gather.12
where the time goes:
time: 480 us; the launch traced here: 478 us
  waiting for transfers between devices  295 us (61%)
  other arithmetic  51.9 us (11%)
  blocking collectives  51.3 us (11%)
  matrix products  31.7 us (7%)
  local copies, waits for them, and re-layouts  27.4 us (6%)
  between operations  16.9 us (4%)
    psum x1, waiting for transfers between devices, body(): lax.psum(partial_value.astype(jnp.bfloat16), 'vocab').astype(jnp.float32)  92.2 us
    all_gather x1, waiting for transfers between devices, head_logits(): lax.all_gather(head_w, 'dp', axis=1, tiled=True)  89.2 us
    all_gather x1, waiting for transfers between devices, body(): lax.all_gather(in_x, 'dp', axis=0, tiled=True)  54.1 us
    all_gather x2, waiting for transfers between devices, prefix(): gathered = jax.tree.map(lambda a: lax.all_gather(a, axis), part)  39.2 us
    psum x1, blocking collectives, body(): lax.psum(jnp.dot(conv_low, xbc_w, preferred_element_type=jnp.float32).ast...  18.7 us
    psum x1, waiting for transfers between devices, body(): lax.psum(jnp.dot(conv_low, xdt_w, preferred_element_type=jnp.float32).ast...  17.4 us
    neg x16, other arithmetic, run_block(): -step_blk[position][..., None] * a_rate  14.9 us
    slice x8, local copies, waits for them, and re-layouts, run_block(): conv_blk[position]  13.3 us
  transfers between devices with their start and end apart: 8, of which 7 were waited for; matrix products, arithmetic and copies ran while one was open for 16% of the time, Pallas kernels for 0%

commit v1 on v0

--- a/solution.py
+++ b/solution.py
@@ -149,7 +149,9 @@
     vocab_index = lax.axis_index("vocab")
     share_width = width // vocab_count
     flat_stream = stream.reshape(row_count, width)
-    mixer_out = lax.psum(partial_value.astype(jnp.bfloat16), "vocab").astype(jnp.float32)
+    mixer_out = jnp.sum(lax.all_gather(partial_value.astype(jnp.bfloat16), "vocab"), axis=0).astype(
+        jnp.float32
+    )
     hidden = (flat_stream + mixer_out).astype(jnp.bfloat16)
     final = rms_norm(hidden.astype(jnp.float32), final_gain, 1e-05).astype(jnp.bfloat16)
     hidden_share = lax.dynamic_slice_in_dim(hidden, vocab_index * share_width, share_width, 1)

time: 480 us -> 542 us (1.13)
  waiting for transfers between devices: 295 us -> 351 us
  other arithmetic: 51.9 us -> 59.9 us
    all_gather x0 -> x1, waiting for transfers between devices: none -> 156 us  [body(): lax.all_gather(partial_value.astype(jnp.bfloat16), 'vocab')]
    psum x1 -> x0, waiting for transfers between devices: 92.2 us -> none  [body(): lax.psum(partial_value.astype(jnp.bfloat16), 'vocab').astype(jnp.float32)]
    all_gather x1, waiting for transfers between devices: 89.2 us -> 81.5 us  [head_logits(): lax.all_gather(head_w, 'dp', axis=1, tiled=True)]
    reduce_sum x0 -> x1, other arithmetic: none -> 6.96 us  [body(): jnp.sum(lax.all_gather(partial_value.astype(jnp.bfloat16), 'vocab'), axis=0)]
  transfers between devices with their start and end apart: 8 -> 8, of which waited for: 7 -> 7; matrix products, arithmetic and copies ran while one was open for 16% -> 15% of each run, Pallas kernels for 0% -> 0%
where the time goes in v1:
time: 542 us; the launch traced here: 540 us
  waiting for transfers between devices  351 us (65%)
  other arithmetic  59.9 us (11%)
  blocking collectives  51.3 us (9%)
  matrix products  31.8 us (6%)
  local copies, waits for them, and re-layouts  26.2 us (5%)
  between operations  16.8 us (3%)
    all_gather x1, waiting for transfers between devices, body(): lax.all_gather(partial_value.astype(jnp.bfloat16), 'vocab')  156 us
    all_gather x1, waiting for transfers between devices, head_logits(): lax.all_gather(head_w, 'dp', axis=1, tiled=True)  81.5 us
    all_gather x1, waiting for transfers between devices, body(): lax.all_gather(in_x, 'dp', axis=0, tiled=True)  54.1 us
    all_gather x2, waiting for transfers between devices, prefix(): gathered = jax.tree.map(lambda a: lax.all_gather(a, axis), part)  39.2 us
    psum x1, blocking collectives, body(): lax.psum(jnp.dot(conv_low, xbc_w, preferred_element_type=jnp.float32).ast...  18.7 us
    psum x1, waiting for transfers between devices, body(): lax.psum(jnp.dot(conv_low, xdt_w, preferred_element_type=jnp.float32).ast...  17.4 us
    neg x16, other arithmetic, run_block(): -step_blk[position][..., None] * a_rate  14.9 us
    slice x8, local copies, waits for them, and re-layouts, run_block(): conv_blk[position]  13.3 us
  transfers between devices with their start and end apart: 8, of which 7 were waited for; matrix products, arithmetic and copies ran while one was open for 15% of the time, Pallas kernels for 0%

profile of v1, /device:TPU:0, one launch (start us, length us, event | category | flops | bytes accessed | tf_op | source)
XLA Modules:
  0.0 540.2 jit_solution(740739931242244088)
XLA Ops:
  8.0 2.1 multiply_reduce_fusion.18
  10.1 2.7 multiply_convert_fusion.1
  12.8 54.1 %all-gather.9.cloned.1.call-done = bf16[4096,1024]{1,0:T(8,128)(2,1)} async-done(((bf16[512,1024]{1,0:T(8,128)(2,1)}), bf16[4096,1024]{1,0:T(8,128)(2,1)}) %all-gather.9.cloned.1.call-update) | async-done | bytes 8388624 | tf_op jit(solution)/shard_map/all_gather | solution.py:67
  66.9 6.4 %convolution_convert_fusion.2 = bf16[256,1024]{1,0:T(8,128)(2,1)S(1)} fusion(bf16[256,4096]{1,0:T(8,128)(2,1)} %bitcast.285, bf16[4096,1024]{1,0:T(8,128)(2,1)} %all-gather.9.cloned.1.call-done), kind=kOutput, calls=%fused_computation.216 | convolution fusion | flops 2147745792 | bytes 11010048 | tf_op jit(solution)/shard_map/dot_general | solution.py:66
  73.3 2.3 collective-permute-start
  75.6 0.8 collective-permute-done
  76.6 1.7 fusion.70
  78.3 1.0 convolution_convert_fusion.3
  80.3 18.7 %psum.36 = bf16[256,32]{0,1:T(8,128)(2,1)S(1)} all-reduce(bf16[256,32]{0,1:T(8,128)(2,1)S(1)} %convolution_convert_fusion.4), channel_id=1, replica_groups=mesh['dp'=8,'vocab'=4] {'vocab'}, use_global_device_ids=true, to_apply=%region_3.4 | all-reduce | flops 8192 | bytes 32768 | tf_op jit(solution)/shard_map/psum | solution.py:86
  99.4 17.4 %all-reduce.3.cloned.1.call-done = bf16[256,256]{1,0:T(8,128)(2,1)} async-done(((bf16[256,256]{1,0:T(8,128)(2,1)}), bf16[256,256]{1,0:T(8,128)(2,1)}) %all-reduce.3.cloned.1.call-update) | async-done | bytes 131088 | tf_op jit(solution)/shard_map/psum | solution.py:82
  116.7 1.0 fusion.62
  117.8 1.8 bitcast_reduce_fusion
  119.6 1.0 copy-done.6
  120.5 1.9 copy.36
  122.4 48.8 %while.26 = (s32[]{:T(128)}, f32[2,1024,16]{1,2,0:T(8,128)S(1)}, f32[8,16,2,1024]{3,1,0,2:T(8,128)}, f32[8,16,2,1024]{3,2,1,0:T(2,128)}, f32[1024,16]{0,1:T(8,12...) while((s32[]{:T(128)}, f32[2,1024,16]{1,2,0:T(8,128)S(1)}, ...), condition=%wide.region_21.22_spmd.clone, body=%wide.region_4.21_spmd.clone.sunk | while | flops 4816914 | bytes 3422816 | solution.py:118
  122.4 1.6 constant_dynamic-slice_fusion.66
  124.0 0.9 negate_bitcast_fusion.18
  125.0 1.0 negate_bitcast_fusion.19
  128.5 1.6 constant_dynamic-slice_fusion.66
  130.2 0.9 negate_bitcast_fusion.18
  131.1 1.0 negate_bitcast_fusion.19
  133.9 0.7 copy_dynamic-update-slice_fusion.2
  134.6 1.6 constant_dynamic-slice_fusion.66
  136.2 0.9 negate_bitcast_fusion.18
  137.1 1.0 negate_bitcast_fusion.19
  140.0 0.7 copy_dynamic-update-slice_fusion.2
  140.7 1.6 constant_dynamic-slice_fusion.66
  142.3 0.9 negate_bitcast_fusion.18
  143.2 1.0 negate_bitcast_fusion.19
  146.0 0.7 copy_dynamic-update-slice_fusion.2
  146.7 1.6 constant_dynamic-slice_fusion.66
  148.3 0.9 negate_bitcast_fusion.18
  149.2 1.0 negate_bitcast_fusion.19
  152.1 0.7 copy_dynamic-update-slice_fusion.2
  152.8 1.6 constant_dynamic-slice_fusion.66
  154.4 0.9 negate_bitcast_fusion.18
  155.3 1.0 negate_bitcast_fusion.19
  158.2 0.7 copy_dynamic-update-slice_fusion.2
  158.8 1.9 constant_dynamic-slice_fusion.66
  160.7 0.9 negate_bitcast_fusion.18
  161.6 1.0 negate_bitcast_fusion.19
  165.2 1.6 constant_dynamic-slice_fusion.66
  166.8 0.9 negate_bitcast_fusion.18
  167.7 1.0 negate_bitcast_fusion.19
  170.5 0.7 copy_dynamic-update-slice_fusion.2
  172.7 6.3 %convolution_convert_fusion.1 = bf16[256,1024]{1,0:T(8,128)(2,1)S(1)} fusion(bf16[256,4096]{1,0:T(8,128)(2,1)} %bitcast.286, bf16[4096,1024]{1,0:T(8,128)(2,1)} %all-gather.13.cloned.1.call-done), kind=kOutput, calls=%fused_computation.215 | convolution fusion | flops 2147745792 | bytes 11010048 | tf_op jit(solution)/shard_map/dot_general | solution.py:69
  179.2 2.7 reduce_window_sum.11
  181.9 2.3 neg.205
  184.3 13.5 %all-gather.17.cloned.1.call-done = f32[16,1024,16]{1,2,0:T(8,128)} async-done(((f32[2,1024,16]{1,2,0:T(8,128)}), f32[16,1024,16]{1,2,0:T(8,128)}) %all-gather.17.cloned.1.call-update) | async-done | bytes 1048592 | tf_op jit(solution)/shard_map/all_gather | solution.py:16
  197.8 25.7 %all-gather.11.cloned.1.call-done = f32[8,2,1024,16]{2,3,1,0:T(8,128)} async-done(((f32[1,2,1024,16]{2,3,1,0:T(8,128)}), f32[8,2,1024,16]{2,3,1,0:T(8,128)}) %all-gather.11.cloned.1.call-update) | async-done | bytes 1048592 | tf_op jit(solution)/shard_map/all_gather | solution.py:16
  223.7 6.2 %multiply_reduce_fusion.16 = f32[2,128,1024]{2,1,0:T(8,128)S(1)} fusion(f32[2,1024,16]{1,2,0:T(8,128)S(1)} %get-tuple-element.92, f32[1024,16]{0,1:T(8,128)S(1)} %get-tuple-element.675, f32[2,128,1024]{2,1,0:T(8,128)} %neg.205, f32[2,128,16]{2,1,0:T(8,128)S(1)} %copy.41), kind=kLoop, calls=%fused_computation.196 | loop fusion | flops 16515072 | bytes 2310144 | tf_op jit(solution)/shard_map/reduce_sum | solution.py:137
  230.3 7.1 %convolution_convert_fusion = bf16[256,4096]{1,0:T(8,128)(2,1)} fusion(bf16[256,1024]{1,0:T(8,128)(2,1)S(1)} %bitcast.291, bf16[1024,4096]{1,0:T(8,128)(2,1)} %param.33), kind=kOutput, calls=%fused_computation.197 | convolution fusion | flops 2148532224 | bytes 11010048 | tf_op jit(solution)/shard_map/dot_general | solution.py:147
  237.5 0.7 all-gather.15.cloned.1.call-update
  238.8 155.7 %all-gather.19.cloned.1.call-done = bf16[1024,4096]{1,0:T(8,128)(2,1)} async-done(((bf16[256,4096]{1,0:T(8,128)(2,1)}), bf16[1024,4096]{1,0:T(8,128)(2,1)}) %all-gather.19.cloned.1.call-update) | async-done | bytes 8388624 | tf_op jit(solution)/shard_map/all_gather | solution.py:152
  394.5 7.0 %reduce_sum.241 = bf16[256,4096]{1,0:T(8,128)(2,1)} reduce(bf16[4,256,4096]{2,1,0:T(8,128)(2,1)} %bitcast.277, bf16[]{:T(256)} %constant.71.clone.1), dimensions={0}, to_apply=%region_27.28 | reduce | flops 3145728 | bytes 10485762 | tf_op jit(solution)/shard_map/reduce_sum | solution.py:152
  401.5 2.9 fusion.49
  404.4 0.9 constant_dynamic-slice_fusion.64
  405.4 0.8 multiply_reduce_fusion.17
  406.2 81.5 %all-gather.15.cloned.1.call-done = bf16[2048,4096]{1,0:T(8,128)(2,1)} async-done(((bf16[2048,512]{1,0:T(8,128)(2,1)}), bf16[2048,4096]{1,0:T(8,128)(2,1)}) %all-gather.15.cloned.1.call-update) | async-done | bytes 16777232 | tf_op jit(solution)/shard_map/all_gather | solution.py:34
  487.6 9.0 %fusion.73 = (f32[256]{0:T(256)S(1)}, f32[256,2048]{1,0:T(8,128)S(1)}) fusion(bf16[2048,4096]{1,0:T(8,128)(2,1)} %all-gather.15.cloned.1.call-done, bf16[256,4096]{1,0:T(8,128)(2,1)} %copy-done.7, f32[4096]{0:T(1024)S(1)} %copy-done.15, f32[256]{0:T(256)S(1)} %rsqrt_bitcast_fusion), kind=kOutput, calls=%fused_computation.258 | convolution fusion | flops 4299685888 | bytes 20989952 | tf_op jit(solution)/shard_map/dot_general | solution.py:32
  496.6 11.7 %pmax.7 = f32[256]{0:T(256)S(1)} all-reduce(f32[256]{0:T(256)S(1)} %get-tuple-element.286), channel_id=1, replica_groups=mesh['dp'=8,'vocab'=4] {'vocab'}, use_global_device_ids=true, to_apply=%region_32.33 | all-reduce | flops 256 | bytes 2048 | tf_op jit(solution)/shard_map/pmax | solution.py:164
  509.0 8.4 %all-reduce = (f32[256]{0:T(256)S(1)}, f32[256]{0:T(256)S(1)}) all-reduce(f32[256]{0:T(256)S(1)} %get-tuple-element.144, f32[256]{0:T(256)S(1)} %get-tuple-element.143), channel_id=1, replica_groups=mesh['dp'=8,'vocab'=4] {'vocab'}, use_global_device_ids=true, to_apply=%region_30.31 | all-reduce | flops 512 | bytes 4096 | tf_op jit(solution)/shard_map/psum | solution.py:166
  517.4 1.2 fusion.68
  518.5 12.4 %psum.39 = f32[]{:T(128)} all-reduce(f32[]{:T(128)} %get-tuple-element.282), channel_id=1, replica_groups=mesh['dp'=8,'vocab'=4] {'dp'}, use_global_device_ids=true, to_apply=%region_36.37 | all-reduce | flops 1 | bytes 8 | tf_op jit(solution)/shard_map/psum | solution.py:172
  (251 shorter events, 21.4 us)
Async XLA Ops:
  7.2 110.6 %copy-start = (bf16[256,1024]{1,0:T(8,128)(2,1)S(1)}, bf16[256,1024]{1,0:T(8,128)(2,1)}, u32[]{:S(2)}) copy-start(bf16[256,1024]{1,0:T(8,128)(2,1)} %param.30) | copy-start | bytes 1572868
  7.2 2.9 copy-start.3
  7.2 59.7 %all-gather.9.cloned.1.call-start = ((), (), s32[]{:S(2)}) async-start(), calls=%async_computation | async-start | bytes 9437184 | tf_op jit(solution)/shard_map/all_gather | solution.py:67
  7.9 108.8 %all-reduce.3.cloned.1.call-start = ((), (), s32[]{:S(2)}) async-start(), calls=%async_computation.1 | async-start | bytes 262144 | tf_op jit(solution)/shard_map/psum | solution.py:82
  66.9 8.7 %copy-start.11 = (f32[4,1024]{1,0:T(4,128)S(1)}, f32[4,1024]{1,0:T(4,128)}, u32[]{:S(2)}) copy-start(f32[4,1024]{1,0:T(4,128)} %param.25) | copy-start | bytes 49156
  66.9 9.7 %copy-start.12 = (f32[1024]{0:T(1024)S(1)}, f32[1024]{0:T(1024)}, u32[]{:S(2)}) copy-start(f32[1024]{0:T(1024)} %param.26) | copy-start | bytes 12292
  73.3 5.0 copy-start.9
  73.3 3.1 collective-permute-start
  76.6 3.5 copy-start.10
  76.6 41.2 %copy-start.16 = (f32[1024]{0:T(1024)S(1)}, f32[1024]{0:T(1024)}, u32[]{:S(2)}) copy-start(f32[1024]{0:T(1024)} %param.31) | copy-start | bytes 12292
  76.6 41.2 %copy-start.17 = (f32[256]{0:T(256)S(1)}, f32[256]{0:T(256)}, u32[]{:S(2)}) copy-start(f32[256]{0:T(256)} %param.29) | copy-start | bytes 3076
  79.3 43.2 %copy-start.2 = (f32[1024,16]{0,1:T(8,128)S(1)}, f32[1024,16]{0,1:T(8,128)}, u32[]{:S(2)}) copy-start(f32[1024,16]{0,1:T(8,128)} %param.32) | copy-start | bytes 196612
  79.3 93.4 %all-gather.13.cloned.1.call-start = ((), (), s32[]{:S(2)}) async-start(), calls=%async_computation.3 | async-start | bytes 9437184 | tf_op jit(solution)/shard_map/all_gather | solution.py:70
  80.0 117.7 %all-gather.17.cloned.1.call-start = ((), (), s32[]{:S(2)}) async-start(), calls=%async_computation.5 | async-start | bytes 1179648 | tf_op jit(solution)/shard_map/all_gather | solution.py:16
  119.6 1.0 copy-start.6
  171.2 0.6 copy-start.5
  171.9 51.6 %all-gather.11.cloned.1.call-start = ((), (), s32[]{:S(2)}) async-start(), calls=%async_computation.2 | async-start | bytes 1179648 | tf_op jit(solution)/shard_map/all_gather | solution.py:16
  172.6 221.9 %all-gather.19.cloned.1.call-start = ((), (), s32[]{:S(2)}) async-start(), calls=%async_computation.6 | async-start | bytes 10485760 | tf_op jit(solution)/shard_map/all_gather | solution.py:152
  223.7 6.3 %copy-start.8 = (f32[8,16,2,1024]{3,1,0,2:T(8,128)S(1)}, f32[8,16,2,1024]{3,1,0,2:T(8,128)}, u32[]{:S(2)}) copy-start(f32[8,16,2,1024]{3,1,0,2:T(8,128)} %get-tuple-element.90) | copy-start | bytes 3145732
  237.4 0.8 copy-start.14
  237.4 1.4 copy-start.13
  237.5 250.2 %all-gather.15.cloned.1.call-start = ((), (), s32[]{:S(2)}) async-start(), calls=%async_computation.4 | async-start | bytes 18874368 | tf_op jit(solution)/shard_map/all_gather | solution.py:34
  401.5 3.9 copy-start.4
  404.4 1.7 copy-start.7
  404.4 83.2 %copy-start.15 = (f32[4096]{0:T(1024)S(1)}, f32[4096]{0:T(1024)}, u32[]{:S(2)}) copy-start(f32[4096]{0:T(1024)} %param.34) | copy-start | bytes 49156
  487.6 44.6 %copy-start.1 = (bf16[256,1024]{1,0:T(8,128)(2,1)S(1)}, bf16[256,1024]{1,0:T(8,128)(2,1)}, u32[]{:S(2)}) copy-start(bf16[256,1024]{1,0:T(8,128)(2,1)} %param.30) | copy-start | bytes 1572868
Sparse Core Ops, SparseCore 0:
  9.9 56.9 all-gather.8
  79.4 37.2 all-reduce.2
  118.6 53.9 all-gather.12
  174.4 23.3 all-gather.16
  200.1 23.3 all-gather.10
  237.6 156.8 all-gather.18
  396.4 91.1 all-gather.14
